TPU v7x, 32 devices: a whole 2x2x4 slice. The times are simulated.
32 devices in a mesh: dp: 8 (over y, x, core), tensor: 4 (over z).
Axes of the slice: x: 2, y: 2, z: 4, core: 2. Of those that a mesh axis runs over, the one named last changes fastest.
Arguments:
- tokens: bfloat16 [2048, 8, 1024], P('tensor', 'dp'), may hold values from -6 to 6
- weights: bfloat16 [1024, 12288], P(None, 'tensor'), may hold values from -0.71 to 0.71
- norms: float32 [4, 1024], replicated, may hold values from -0.75 to 1.5
- cotangent: bfloat16 [2048, 8, 1024], P('tensor', 'dp'), may hold values from -6 to 6
- lengths: int32 [8], P('dp'), may hold values from 512 to 2048, as said below
- owners: int32 [7], replicated, may hold values from 0 to 7, as said below
- master: float32 [8, 1024, 4096], P('dp', None, 'tensor'), may hold values from -0.05 to 0.05
- moment_one: float32 [8, 1024, 4096], P('dp', None, 'tensor'), may hold values from -24 to 24
- moment_two: float32 [8, 1024, 4096], P('dp', None, 'tensor'), may hold values from 0.5 to 8
- norm_master: float32 [8, 4, 1024], P('dp'), may hold values from 0.5 to 1.5
- norm_one: float32 [8, 4, 1024], P('dp'), may hold values from -24 to 24
- norm_two: float32 [8, 4, 1024], P('dp'), may hold values from 0.5 to 8
Outputs:
- outputs: bfloat16 [2048, 8, 1024], P('tensor', 'dp')
- input_grad: bfloat16 [2048, 8, 1024], P('tensor', 'dp')
- weight_grads: float32 [8, 1024, 4096], P('dp', None, 'tensor')
- new_master: float32 [8, 1024, 4096], P('dp', None, 'tensor')
- new_one: float32 [8, 1024, 4096], P('dp', None, 'tensor')
- new_two: float32 [8, 1024, 4096], P('dp', None, 'tensor')
- new_weights: bfloat16 [1024, 12288], P(None, 'tensor')
- norm_grads: float32 [4, 1024], replicated
- new_norm_master: float32 [8, 4, 1024], P('dp')
- new_norm_one: float32 [8, 4, 1024], P('dp')
- new_norm_two: float32 [8, 4, 1024], P('dp')
Inputs may be any that keep to these rules, and one draw needn't show every extreme that they name: `lengths`: some sequence fills all 2048 positions. The up and down matrices have different owners that own no other matrix; the four attention matrices have at most two owners between them, neither of them an owner of up or down, so no index owns more than 4 tiles of a block and the owner of up owns exactly 4.
All inputs are finite; a program needn't handle non-finite values.
Results may differ from a plain program's by a relative error of at most 0.02.
Values may be sent and summed in bfloat16 or wider, within the bound.
A program may use at most 192 MiB of HBM per device.

v0:
```python
from functools import partial
import jax
import jax.numpy as jnp
from jax import lax
from jax.sharding import PartitionSpec as P

D = 1024
FF = 4096
ADAM_STEP = 10
HEAD_DIM = 64
precise = lax.Precision.HIGHEST
beta_one = 0.9
beta_two = 0.999
learn_rate = 0.02
weight_decay = 0.1
adam_eps = 1e-08
norm_eps = 1e-05
masked_score = -1e30


def layer_norm_parts(value, gain, shift):
    average = jnp.mean(value, axis=-1, keepdims=True)
    centred = value - average
    variance = jnp.mean(centred * centred, axis=-1, keepdims=True)
    inverse = lax.rsqrt(variance + norm_eps)
    normed = centred * inverse
    return (normed * gain + shift, normed, inverse)


def layer_norm_back(upstream, normed, inverse, gain):
    scaled = upstream * gain
    inner = (
        scaled
        - jnp.mean(scaled, axis=-1, keepdims=True)
        - normed * jnp.mean(scaled * normed, axis=-1, keepdims=True)
    )
    return (inner * inverse, jnp.sum(upstream * normed, axis=0), jnp.sum(upstream, axis=0))


def slot_table(owners):
    repeat = FF // D
    tile_matrix = jnp.array([0, 1, 2, 3] + [4] * repeat + [5] * repeat, dtype=jnp.int32)
    choose = (tile_matrix[:, None] == jnp.arange(7, dtype=jnp.int32)[None, :]).astype(jnp.int32)
    tile_owner = jnp.sum(choose * owners[None, :], axis=1)
    position = jnp.arange(tile_matrix.shape[0], dtype=jnp.int32)
    before = (tile_owner[None, :] == tile_owner[:, None]) & (position[None, :] < position[:, None])
    slot_index = jnp.sum(before.astype(jnp.int32), axis=1)
    return (tile_owner, slot_index)


def adam_update(grad, param, first, second, occupied, decay_rate):
    first_new = occupied * (beta_one * first + (1.0 - beta_one) * grad)
    second_new = occupied * (beta_two * second + (1.0 - beta_two) * grad * grad)
    correct_one = 1.0 - beta_one**ADAM_STEP
    correct_two = 1.0 - beta_two**ADAM_STEP
    direction = first_new / correct_one / (jnp.sqrt(second_new / correct_two) + adam_eps)
    param_new = occupied * (param - learn_rate * (direction + decay_rate * param))
    return (param_new, first_new, second_new)


def collect(row_shard):
    return lax.all_gather(row_shard, "tensor", axis=0, tiled=True)


def spread_rows(term, row_count):
    return lax.psum_scatter(
        term(jnp.int32(0), row_count * lax.axis_size("tensor")).astype(jnp.bfloat16),
        "tensor",
        scatter_dimension=0,
        tiled=True,
    ).astype(jnp.float32)


def row_product(source, weight, form):

    def term(row_start, row_total):
        return jnp.einsum(form, source, weight, preferred_element_type=jnp.float32)

    return term


def scored(query_block, key_rows, present):
    score_scale = HEAD_DIM ** (-0.5)
    scores = (
        jnp.einsum("qhe,khe->hqk", query_block, key_rows, preferred_element_type=jnp.float32)
        * score_scale
    )
    return jnp.where(present[None, None, :], scores, masked_score)


def attention_forward(queries, key_rows, value_rows, present):
    seq_len, heads_here, head_size = queries.shape
    block_rows = min(512, seq_len)

    def block_forward(query_block):
        scores = scored(query_block, key_rows, present)
        maxima = jnp.max(scores, axis=-1, keepdims=True)
        exponent = jnp.exp(scores - maxima)
        totals = jnp.sum(exponent, axis=-1, keepdims=True)
        attention = (exponent / totals).astype(jnp.bfloat16)
        context = jnp.einsum(
            "hqk,khe->qhe", attention, value_rows, preferred_element_type=jnp.float32
        )
        return (context.astype(jnp.bfloat16), (maxima + jnp.log(totals))[:, :, 0])

    return lax.map(
        block_forward, queries.reshape(seq_len // block_rows, block_rows, heads_here, head_size)
    )


def attention_backward(queries, key_rows, value_rows, present, logsum, context_grad):
    seq_len, heads_here, head_size = queries.shape
    block_rows = min(512, seq_len)
    count_blocks = seq_len // block_rows
    score_scale = HEAD_DIM ** (-0.5)

    def block_backward(running, block_items):
        key_grad, value_grad = running
        query_block, logsum_block, upstream = block_items
        attention = jnp.exp(scored(query_block, key_rows, present) - logsum_block[:, :, None])
        product = jnp.einsum(
            "qhe,khe->hqk", upstream, value_rows, preferred_element_type=jnp.float32
        )
        score_grad = (
            attention * (product - jnp.sum(attention * product, axis=-1, keepdims=True))
        ).astype(jnp.bfloat16)
        query_grad = (
            jnp.einsum("hqk,khe->qhe", score_grad, key_rows, preferred_element_type=jnp.float32)
            * score_scale
        ).astype(jnp.bfloat16)
        key_grad = (
            key_grad
            + jnp.einsum(
                "hqk,qhe->khe", score_grad, query_block, preferred_element_type=jnp.float32
            )
            * score_scale
        )
        value_grad = value_grad + jnp.einsum(
            "hqk,qhe->khe",
            attention.astype(jnp.bfloat16),
            upstream,
            preferred_element_type=jnp.float32,
        )
        return ((key_grad, value_grad), query_grad)

    start_grads = (jnp.zeros(key_rows.shape, jnp.float32), jnp.zeros(value_rows.shape, jnp.float32))
    blocked = (
        queries.reshape(count_blocks, block_rows, heads_here, head_size),
        logsum,
        context_grad.reshape(count_blocks, block_rows, heads_here, head_size),
    )
    (key_grad, value_grad), query_grad = lax.scan(block_backward, start_grads, blocked)
    flat_width = heads_here * head_size
    return (
        query_grad.reshape(seq_len, flat_width),
        key_grad.astype(jnp.bfloat16).reshape(seq_len, flat_width),
        value_grad.astype(jnp.bfloat16).reshape(seq_len, flat_width),
    )


def local(
    tokens,
    weights,
    norms,
    cotangent,
    lengths,
    owners,
    master,
    moment_one,
    moment_two,
    norm_master,
    norm_one,
    norm_two,
):
    tensor_size = lax.axis_size("tensor")
    group_size = lax.axis_size("dp")
    tile_width = D // tensor_size
    hidden_width = FF // tensor_size
    heads_here = tile_width // HEAD_DIM
    row_count = tokens.shape[0]
    seq_len = row_count * tensor_size
    w_mixed = weights[:, : 3 * tile_width]
    w_out = weights[:, 3 * tile_width : 4 * tile_width]
    w_up = weights[:, 4 * tile_width : 4 * tile_width + hidden_width]
    w_down = weights[:, 4 * tile_width + hidden_width :]
    length = lengths[0]
    present = jnp.arange(seq_len) < length
    own_present = lax.axis_index("tensor") * row_count + jnp.arange(row_count) < length
    inputs = tokens[:, 0, :]
    gathered = collect(inputs)
    mixed = jnp.dot(gathered, w_mixed, preferred_element_type=jnp.float32).astype(jnp.bfloat16)
    mixed = mixed.reshape(seq_len, 3, heads_here, HEAD_DIM)
    context, logsum = attention_forward(mixed[:, 0], mixed[:, 1], mixed[:, 2], present)
    context = context.reshape(seq_len, tile_width)
    branch = spread_rows(row_product(context, w_out, "se,de->sd"), row_count)
    first_norm, first_normed, first_inverse = layer_norm_parts(
        inputs.astype(jnp.float32) + branch, norms[0], norms[1]
    )
    first_low = first_norm.astype(jnp.bfloat16)
    gathered_first = collect(first_low)
    hidden_pre = jnp.dot(gathered_first, w_up, preferred_element_type=jnp.float32)
    hidden_pre, hidden = (
        hidden_pre,
        jax.nn.gelu(hidden_pre, approximate=False).astype(jnp.bfloat16),
    )
    feed = spread_rows(row_product(hidden, w_down, "sf,df->sd"), row_count)
    second_norm, second_normed, second_inverse = layer_norm_parts(
        first_norm + feed, norms[2], norms[3]
    )
    seed_grad = cotangent[:, 0, :].astype(jnp.float32) * own_present[:, None].astype(jnp.float32)
    second_grad, gain_two, shift_two = layer_norm_back(
        seed_grad, second_normed, second_inverse, norms[2]
    )
    feed_low = second_grad.astype(jnp.bfloat16)
    gathered_feed = collect(feed_low)
    hidden_grad = jnp.dot(gathered_feed, w_down, preferred_element_type=jnp.float32)
    gelu_back = jax.vjp(partial(jax.nn.gelu, approximate=False), hidden_pre)[1]
    pre_grad = gelu_back(hidden_grad)[0].astype(jnp.bfloat16)
    down_grad = jnp.einsum("sd,sf->df", gathered_feed, hidden, preferred_element_type=jnp.float32)
    up_grad = jnp.einsum("sd,sf->df", gathered_first, pre_grad, preferred_element_type=jnp.float32)
    first_grad = second_grad + spread_rows(row_product(pre_grad, w_up, "sf,df->sd"), row_count)
    branch_grad, gain_one, shift_one = layer_norm_back(
        first_grad, first_normed, first_inverse, norms[0]
    )
    branch_low = branch_grad.astype(jnp.bfloat16)
    gathered_branch = collect(branch_low)
    context_grad = jnp.dot(gathered_branch, w_out, preferred_element_type=jnp.float32).astype(
        jnp.bfloat16
    )
    out_grad = jnp.einsum("sd,se->de", gathered_branch, context, preferred_element_type=jnp.float32)
    query_grad, key_grad, value_grad = attention_backward(
        mixed[:, 0], mixed[:, 1], mixed[:, 2], present, logsum, context_grad
    )
    mixed_grad = jnp.concatenate([query_grad, key_grad, value_grad], axis=1)
    mixed_weight_grad = jnp.einsum(
        "sd,se->de", gathered, mixed_grad, preferred_element_type=jnp.float32
    )
    input_total = branch_grad + spread_rows(
        row_product(mixed_grad, w_mixed, "se,de->sd"), row_count
    )
    input_grad = input_total.astype(jnp.bfloat16)[:, None, :]
    mixed_weight_grad, out_grad, up_grad, down_grad = (
        lax.psum_scatter(mixed_weight_grad, "dp", scatter_dimension=0, tiled=True),
        lax.psum_scatter(out_grad, "dp", scatter_dimension=0, tiled=True),
        lax.psum_scatter(up_grad, "dp", scatter_dimension=0, tiled=True),
        lax.psum_scatter(down_grad, "dp", scatter_dimension=0, tiled=True),
    )
    packed_grad = jnp.concatenate([mixed_weight_grad, out_grad, up_grad, down_grad], axis=1)
    norm_grads = lax.psum(jnp.stack([gain_one, shift_one, gain_two, shift_two]), ("dp", "tensor"))
    device = lax.axis_index("dp")
    tile_owner, slot_index = slot_table(owners)
    capacity = FF // D
    slot_ids = jnp.arange(capacity, dtype=jnp.int32)
    owned = ((tile_owner[None, :] == device) & (slot_index[None, :] == slot_ids[:, None])).astype(
        jnp.float32
    )
    occupied = jnp.sum(owned, axis=1)[None, :, None]
    share_rows = D // group_size
    everyone = jnp.arange(group_size, dtype=jnp.int32)
    owned_every = (
        (tile_owner[None, None, :] == everyone[:, None, None])
        & (slot_index[None, None, :] == slot_ids[None, :, None])
    ).astype(jnp.float32)
    share_tiles = packed_grad.reshape(share_rows, -1, tile_width)
    outgoing = jnp.einsum("xiw,psi->pxsw", share_tiles, owned_every, precision=precise)
    incoming = lax.all_to_all(
        outgoing.astype(jnp.bfloat16), "dp", split_axis=0, concat_axis=0, tiled=True
    ).astype(outgoing.dtype)
    slot_grad = incoming.reshape(D, capacity, tile_width)
    new_master, new_one, new_two = adam_update(
        slot_grad,
        master[0].reshape(D, capacity, tile_width),
        moment_one[0].reshape(D, capacity, tile_width),
        moment_two[0].reshape(D, capacity, tile_width),
        occupied,
        weight_decay,
    )
    rounded_low = new_master.astype(jnp.bfloat16).reshape(
        group_size, share_rows, capacity, tile_width
    )
    returned = lax.all_to_all(rounded_low, "dp", split_axis=0, concat_axis=0, tiled=True)
    placed = jnp.einsum(
        "pxsw,psi->xiw", returned.astype(jnp.float32), owned_every, precision=precise
    )
    row_shard = placed.astype(jnp.bfloat16).reshape(share_rows, -1)
    new_weights = lax.all_gather(row_shard, "dp", axis=0, tiled=True)
    norm_owner = (device == owners[6]).astype(jnp.float32)
    new_norm_master, new_norm_one, new_norm_two = adam_update(
        norm_grads, norm_master[0], norm_one[0], norm_two[0], norm_owner, 0.0
    )
    store_shape = (1, D, capacity * tile_width)
    return (
        second_norm.astype(jnp.bfloat16)[:, None, :],
        input_grad,
        slot_grad.reshape(store_shape),
        new_master.reshape(store_shape),
        new_one.reshape(store_shape),
        new_two.reshape(store_shape),
        new_weights,
        norm_grads,
        new_norm_master[None],
        new_norm_one[None],
        new_norm_two[None],
    )


def solution(mesh):
    in_specs = (
        P("tensor", "dp", None),
        P(None, "tensor"),
        P(),
        P("tensor", "dp", None),
        P("dp"),
        P(),
        P("dp", None, "tensor"),
        P("dp", None, "tensor"),
        P("dp", None, "tensor"),
        P("dp", None, None),
        P("dp", None, None),
        P("dp", None, None),
    )
    out_specs = (
        P("tensor", "dp", None),
        P("tensor", "dp", None),
        P("dp", None, "tensor"),
        P("dp", None, "tensor"),
        P("dp", None, "tensor"),
        P("dp", None, "tensor"),
        P(None, "tensor"),
        P(),
        P("dp", None, None),
        P("dp", None, None),
        P("dp", None, None),
    )
    return jax.shard_map(local, mesh=mesh, in_specs=in_specs, out_specs=out_specs, check_vma=False)
```

profile of v0, /device:TPU:0, one launch (start us, length us, event | category | flops | bytes accessed | tf_op | source)
XLA Modules:
  0.0 1279.9 jit_solution(14837155289518703411)
XLA Ops:
  8.0 85.1 %all-gather.15.cloned.1.call-done = bf16[2048,1,1024]{2,0,1:T(8,128)(2,1)} async-done(((bf16[512,1,1024]{2,0,1:T(8,128)(2,1)}), bf16[2048,1,1024]{2,0,1:T(8,128)(2,1)}) %all-gather.15.cloned.1.call-update) | async-done | bytes 4194320 | tf_op jit(solution)/shard_map/all_gather | solution.py:62
  103.6 50.0 %while.28 = (s32[]{:T(128)}, bf16[4,512,4,64]{1,3,2,0:T(8,128)(2,1)}, f32[4,4,512]{2,1,0:T(4,128)S(1)}, bf16[4,512,4,64]{1,3,2,0:T(8,128)(2,1)S(1)}, bf16[2048,4...) while((s32[]{:T(128)}, ...), condition=%wide.region_3.4_spmd.clone, body=%wide.region_0.3_spmd.clone.sunk | while | flops 1124204544 | bytes 53026924 | solution.py:106
  162.8 74.7 %reduce-scatter.9.cloned.1.call-done = bf16[512,1024]{1,0:T(8,128)(2,1)} async-done(((bf16[2048,1024]{1,0:T(8,128)(2,1)}), bf16[512,1024]{1,0:T(8,128)(2,1)}) %reduce-scatter.9.cloned.1.call-update) | async-done | bytes 1048592 | tf_op jit(solution)/shard_map/reduce_scatter | solution.py:66
  242.5 81.4 %all-gather.7.cloned.1.call-done = bf16[2048,1024]{1,0:T(8,128)(2,1)} async-done(((bf16[512,1024]{1,0:T(8,128)(2,1)}), bf16[2048,1024]{1,0:T(8,128)(2,1)}) %all-gather.7.cloned.1.call-update) | async-done | bytes 4194320 | tf_op jit(solution)/shard_map/all_gather | solution.py:62
  323.9 25.6 %multiply_convert_fusion.1 = (bf16[2048,1024]{1,0:T(8,128)(2,1)S(1)}, f32[2048,1024]{1,0:T(8,128)}, f32[2048,1024]{1,0:T(8,128)}) fusion(bf16[2048,1024]{1,0:T(8,128)(2,1)} %all-gather.7.cloned.1.call-done, bf16[1024,3072]{1,0:T(8,128)(2,1)} %param.18), kind=kOutput, calls=%fused_computation.55 | convolution fusion | flops 4431282176 | bytes 27262976 | tf_op jit(solution)/shard_map/dot_general | solution.py:201
  359.8 74.7 %reduce-scatter.11.cloned.1.call-done = bf16[512,1024]{1,0:T(8,128)(2,1)} async-done(((bf16[2048,1024]{1,0:T(8,128)(2,1)}), bf16[512,1024]{1,0:T(8,128)(2,1)}) %reduce-scatter.11.cloned.1.call-update) | async-done | bytes 1048592 | tf_op jit(solution)/shard_map/reduce_scatter | solution.py:66
  441.5 81.1 %all-gather.9.cloned.1.call-done = bf16[2048,1024]{1,0:T(8,128)(2,1)} async-done(((bf16[512,1024]{1,0:T(8,128)(2,1)}), bf16[2048,1024]{1,0:T(8,128)(2,1)}) %all-gather.9.cloned.1.call-update) | async-done | bytes 4194320 | tf_op jit(solution)/shard_map/all_gather | solution.py:62
  522.7 13.7 %add_convert_fusion = bf16[2048,1024]{1,0:T(8,128)(2,1)S(1)} fusion(f32[2048,1024]{1,0:T(8,128)} %get-tuple-element.307, f32[2048,1024]{1,0:T(8,128)} %get-tuple-element.325, bf16[2048,1024]{1,0:T(8,128)(2,1)} %all-gather.9.cloned.1.call-done, bf16[1024,3072]{1,0:T(8,128)(2,1)} %param.18), kind=kOutput, calls=%fused_computation.54 | convolution fusion | flops 4324327424 | bytes 27262976 | tf_op jit(solution)/shard_map/dot_general | solution.py:216
  546.1 75.4 %reduce-scatter.13.cloned.1.call-done = bf16[512,1024]{1,0:T(8,128)(2,1)} async-done(((bf16[2048,1024]{1,0:T(8,128)(2,1)}), bf16[512,1024]{1,0:T(8,128)(2,1)}) %reduce-scatter.13.cloned.1.call-update) | async-done | bytes 1048592 | tf_op jit(solution)/shard_map/reduce_scatter | solution.py:66
  627.9 81.3 %all-gather.11.cloned.1.call-done = bf16[2048,1024]{1,0:T(8,128)(2,1)} async-done(((bf16[512,1024]{1,0:T(8,128)(2,1)}), bf16[2048,1024]{1,0:T(8,128)(2,1)}) %all-gather.11.cloned.1.call-update) | async-done | bytes 4194320 | tf_op jit(solution)/shard_map/all_gather | solution.py:62
  723.4 166.8 %while.29 = (s32[]{:T(128)}, f32[2048,4,64]{0,2,1:T(8,128)}, f32[2048,4,64]{0,2,1:T(8,128)}, bf16[4,512,4,64]{1,3,2,0:T(8,128)(2,1)}, bf16[4,512,4,64]{1,3,2,0:T...) while((s32[]{:T(128)}, f32[2048,4,64]{0,2,1:T(8,128)}, ...), condition=%wide.region_17.18_spmd.clone, body=%wide.region_15.17_spmd.clone.sunk | while | flops 2750152704 | bytes 172294320 | solution.py:152
  743.1 10.6 multiply_convert_fusion.4
  784.2 10.6 multiply_convert_fusion.4
  826.0 10.6 multiply_convert_fusion.4
  867.9 10.6 multiply_convert_fusion.4
  900.7 10.0 fusion.137
  911.0 10.2 fusion.138
  935.5 9.8 reduce-scatter.17.cloned.1.call-done
  946.5 53.9 %reduce-scatter.21.cloned.1.call-done = f32[128,1024]{1,0:T(8,128)} async-done(((f32[1024,1024]{1,0:T(8,128)}), f32[128,1024]{1,0:T(8,128)}) %reduce-scatter.21.cloned.1.call-update) | async-done | bytes 524304 | tf_op jit(solution)/shard_map/reduce_scatter | solution.py:245
  1000.5 55.0 %reduce-scatter.23.cloned.1.call-done = f32[128,1024]{1,0:T(8,128)} async-done(((f32[1024,1024]{1,0:T(8,128)}), f32[128,1024]{1,0:T(8,128)}) %reduce-scatter.23.cloned.1.call-update) | async-done | bytes 524304 | tf_op jit(solution)/shard_map/reduce_scatter | solution.py:246
  1055.4 39.7 %reduce-scatter.19.cloned.1.call-done = f32[128,256]{1,0:T(8,128)} async-done(((f32[1024,256]{1,0:T(8,128)}), f32[128,256]{1,0:T(8,128)}) %reduce-scatter.19.cloned.1.call-update) | async-done | bytes 131088 | tf_op jit(solution)/shard_map/reduce_scatter | solution.py:244
  1140.8 12.7 subtract_multiply_fusion
  1164.5 30.6 %all_to_all.10 = bf16[8,128,4,256]{3,1,2,0:T(8,128)(2,1)S(1)} all-to-all(bf16[8,128,4,256]{3,1,2,0:T(8,128)(2,1)S(1)} %copy.93), channel_id=1, replica_groups=mesh['dp'=8,'tensor'=4] {'dp'}, dimensions={0} | all-to-all | bytes 4194304 | tf_op jit(solution)/shard_map/all_to_all | solution.py:281
  1199.3 40.5 %psum.7 = f32[4,1024]{1,0:T(4,128)S(1)} all-reduce(f32[4,1024]{1,0:T(4,128)S(1)} %pad_maximum_fusion.4), channel_id=1, replica_groups=mesh['dp'=8,'tensor'=4] {'dp','tensor'}, use_global_device_ids=true, to_apply=%region_30.31 | all-reduce | flops 4096 | bytes 32768 | tf_op jit(solution)/shard_map/psum | solution.py:249
  (220 shorter events, 365.3 us)
Async XLA Ops:
  7.2 85.9 %all-gather.15.cloned.1.call-start = ((), (), s32[]{:S(2)}) async-start(), calls=%async_computation.22 | async-start | bytes 5242880 | tf_op jit(solution)/shard_map/all_gather | solution.py:62
  7.9 229.6 %reduce-scatter.9.cloned.1.call-start = ((), (), s32[]{:S(2)}) async-start(), calls=%async_computation.10 | async-start | bytes 5242880 | tf_op jit(solution)/shard_map/reduce_scatter | solution.py:66
  153.6 8.5 copy-start.6
  162.1 75.4 %copy-start.2 = (bf16[512,1,1024]{2,0,1:T(8,128)(2,1)S(1)}, bf16[512,1,1024]{2,0,1:T(8,128)(2,1)}, u32[]{:S(2)}) copy-start(bf16[512,1,1024]{2,0,1:T(8,128)(2,1)} %param.17) | copy-start | bytes 3145732
  162.1 161.8 %all-gather.7.cloned.1.call-start = ((), (), s32[]{:S(2)}) async-start(), calls=%async_computation.11 | async-start | bytes 5242880 | tf_op jit(solution)/shard_map/all_gather | solution.py:62
  242.4 192.1 %reduce-scatter.11.cloned.1.call-start = ((), (), s32[]{:S(2)}) async-start(), calls=%async_computation.12 | async-start | bytes 5242880 | tf_op jit(solution)/shard_map/reduce_scatter | solution.py:66
  359.1 163.5 %all-gather.9.cloned.1.call-start = ((), (), s32[]{:S(2)}) async-start(), calls=%async_computation.13 | async-start | bytes 5242880 | tf_op jit(solution)/shard_map/all_gather | solution.py:62
  441.3 180.2 %reduce-scatter.13.cloned.1.call-start = ((), (), s32[]{:S(2)}) async-start(), calls=%async_computation.14 | async-start | bytes 5242880 | tf_op jit(solution)/shard_map/reduce_scatter | solution.py:66
  546.0 163.2 %all-gather.11.cloned.1.call-start = ((), (), s32[]{:S(2)}) async-start(), calls=%async_computation.15 | async-start | bytes 5242880 | tf_op jit(solution)/shard_map/all_gather | solution.py:62
  627.8 317.5 %reduce-scatter.17.cloned.1.call-start = ((), (), s32[]{:S(2)}) async-start(), calls=%async_computation.17 | async-start | bytes 3538944 | tf_op jit(solution)/shard_map/reduce_scatter | solution.py:243
  713.8 9.6 copy-start.4
  900.7 99.8 %reduce-scatter.21.cloned.1.call-start = ((), (), s32[]{:S(2)}) async-start(), calls=%async_computation.19 | async-start | bytes 4718592 | tf_op jit(solution)/shard_map/reduce_scatter | solution.py:245
  910.8 144.7 %reduce-scatter.23.cloned.1.call-start = ((), (), s32[]{:S(2)}) async-start(), calls=%async_computation.20 | async-start | bytes 4718592 | tf_op jit(solution)/shard_map/reduce_scatter | solution.py:246
  921.3 173.9 %reduce-scatter.19.cloned.1.call-start = ((), (), s32[]{:S(2)}) async-start(), calls=%async_computation.18 | async-start | bytes 1179648 | tf_op jit(solution)/shard_map/reduce_scatter | solution.py:244
  927.0 335.0 %reduce-scatter.15.cloned.1.call-start = ((), (), s32[]{:S(2)}) async-start(), calls=%async_computation.16 | async-start | bytes 5242880 | tf_op jit(solution)/shard_map/reduce_scatter | solution.py:66
  1104.0 31.0 %all-to-all-start = ((bf16[8,128,4,256]{3,1,2,0:T(8,128)(2,1)}), bf16[8,128,4,256]{3,1,2,0:T(8,128)(2,1)}, u32[]{:S(2)}, u32[]{:S(2)}) async-start(bf16[8,128,4,256]{3,1,2,0:T(8,128)(2,1)} %copy.86), calls=%async_computation.8 | async-start | bytes 4194304 | tf_op jit(solution)/shard_map/all_to_all | solution.py:266
  1108.3 156.2 %all-gather.13.cloned.1.call-start = ((), (), s32[]{:S(2)}) async-start(), calls=%async_computation.21 | async-start | bytes 7077888 | tf_op jit(solution)/shard_map/all_gather | solution.py:286
  1164.4 34.8 %copy-start.16 = (f32[1024]{0:T(1024)S(1)}, f32[1024]{0:T(1024)}, u32[]{:S(2)}) copy-start(f32[1024]{0:T(1024)} %get-tuple-element.257) | copy-start | bytes 12292
  1164.4 34.8 %copy-start.17 = (f32[1024]{0:T(1024)S(1)}, f32[1024]{0:T(1024)}, u32[]{:S(2)}) copy-start(f32[1024]{0:T(1024)} %get-tuple-element.262) | copy-start | bytes 12292
  1164.4 34.8 %copy-start.22 = (f32[1024]{0:T(1024)S(1)}, f32[1024]{0:T(1024)}, u32[]{:S(2)}) copy-start(f32[1024]{0:T(1024)} %get-tuple-element.255) | copy-start | bytes 12292
  1164.4 34.8 %copy-start.23 = (f32[1024]{0:T(1024)S(1)}, f32[1024]{0:T(1024)}, u32[]{:S(2)}) copy-start(f32[1024]{0:T(1024)} %get-tuple-element.260) | copy-start | bytes 12292
  1164.4 75.3 %copy-start.18 = (f32[1,4,1024]{2,1,0:T(4,128)S(1)}, f32[1,4,1024]{2,1,0:T(4,128)}, u32[]{:S(2)}) copy-start(f32[1,4,1024]{2,1,0:T(4,128)} %param.28) | copy-start | bytes 49156
  1164.4 75.3 %copy-start.19 = (f32[1,4,1024]{2,1,0:T(4,128)S(1)}, f32[1,4,1024]{2,1,0:T(4,128)}, u32[]{:S(2)}) copy-start(f32[1,4,1024]{2,1,0:T(4,128)} %param.27) | copy-start | bytes 49156
  1164.4 75.3 %copy-start.20 = (f32[1,4,1024]{2,1,0:T(4,128)S(1)}, f32[1,4,1024]{2,1,0:T(4,128)}, u32[]{:S(2)}) copy-start(f32[1,4,1024]{2,1,0:T(4,128)} %param.26) | copy-start | bytes 49156
  (22 other events, 74.5 us)
Sparse Core Ops, SparseCore 0:
  9.6 83.4 all-gather.14
  162.2 75.2 reduce-scatter.8
  242.6 81.2 all-gather.6
  359.2 75.2 reduce-scatter.10
  441.4 81.2 all-gather.8
  546.2 75.2 reduce-scatter.12
  628.0 81.2 all-gather.10
  900.8 44.5 reduce-scatter.16
  949.3 51.1 reduce-scatter.20
  1004.2 51.1 reduce-scatter.22
  1059.2 35.9 reduce-scatter.18
  1097.9 76.7 reduce-scatter.14
  1198.1 46.6 all-gather.12
where the time goes:
time: 1290 us; the launch traced here: 1280 us
  waiting for transfers between devices  713 us (55%)
  matrix products  263 us (20%)
  other arithmetic  105 us (8%)
  local copies, waits for them, and re-layouts  104 us (8%)
  blocking collectives  71.1 us (6%)
  between operations  15.8 us (1%)
    all_gather x4, waiting for transfers between devices, collect(): return lax.all_gather(row_shard, 'tensor', axis=0, tiled=True)  329 us
    reduce_scatter x4, waiting for transfers between devices, spread_rows(): lax.psum_scatter(term(jnp.int32(0), row_count * lax.axis_size('tensor'))....  225 us
    unnamed x72, local copies, waits for them, and re-layouts  63.2 us
    reduce_scatter x1, waiting for transfers between devices, local(): lax.psum_scatter(down_grad, 'dp', scatter_dimension=0, tiled=True)  55 us
    reduce_scatter x1, waiting for transfers between devices, local(): lax.psum_scatter(up_grad, 'dp', scatter_dimension=0, tiled=True)  53.9 us
    convert_element_type x4, other arithmetic, block_backward(): score_grad = (attention * (product - jnp.sum(attention * product, axis=-1...  42.5 us
    psum x1, blocking collectives, local(): lax.psum(jnp.stack([gain_one, shift_one, gain_two, shift_two]), ('dp', 't...  40.5 us
    reduce_scatter x1, waiting for transfers between devices, local(): lax.psum_scatter(out_grad, 'dp', scatter_dimension=0, tiled=True)  39.7 us
  transfers between devices with their start and end apart: 14, of which 12 were waited for; matrix products, arithmetic and copies ran while one was open for 10% of the time, Pallas kernels for 0%

commit v1 on v0

--- a/solution.py
+++ b/solution.py
@@ -18,6 +18,22 @@
 masked_score = -1e30
 
 
+def ring_gather(x, axis, dim):
+    ways, here, step = (lax.axis_size(axis), lax.axis_index(axis), x.shape[dim])
+    shape = [n * ways if d == dim else n for d, n in enumerate(x.shape)]
+    full = lax.dynamic_update_slice_in_dim(jnp.zeros(shape, x.dtype), x, here * step, axis=dim)
+    going_up = going_down = x
+    for far in range(1, ways // 2 + 1):
+        going_up = lax.ppermute(going_up, axis, [(d, (d + 1) % ways) for d in range(ways)])
+        full = lax.dynamic_update_slice_in_dim(full, going_up, (here - far) % ways * step, axis=dim)
+        if 2 * far < ways:
+            going_down = lax.ppermute(going_down, axis, [(d, (d - 1) % ways) for d in range(ways)])
+            full = lax.dynamic_update_slice_in_dim(
+                full, going_down, (here + far) % ways * step, axis=dim
+            )
+    return full
+
+
 def layer_norm_parts(value, gain, shift):
     average = jnp.mean(value, axis=-1, keepdims=True)
     centred = value - average
@@ -59,7 +75,7 @@
 
 
 def collect(row_shard):
-    return lax.all_gather(row_shard, "tensor", axis=0, tiled=True)
+    return ring_gather(row_shard, "tensor", 0)
 
 
 def spread_rows(term, row_count):

time: 1290 us -> 1110 us (0.86)
  waiting for transfers between devices: 713 us -> 452 us
  starting transfers between devices: 6.2 us -> 82.5 us
    all_gather x4 -> x0, waiting for transfers between devices: 329 us -> none  [collect(): return lax.all_gather(row_shard, 'tensor', axis=0, tiled=True)]
    ppermute x0 -> x12, waiting for transfers between devices: none -> 206 us  [the longest x8 181 us: ring_gather(): lax.ppermute(going_up, axis, [(d, (d + 1) % ways) for d in range(ways)])]
    ppermute x0 -> x12, starting transfers between devices: none -> 77 us  [the longest x8 67.9 us: ring_gather(): lax.ppermute(going_up, axis, [(d, (d + 1) % ways) for d in range(ways)])]
    reduce_scatter x1, waiting for transfers between devices: 55 us -> 0.02 us  [local(): lax.psum_scatter(down_grad, 'dp', scatter_dimension=0, tiled=True)]
    reduce_scatter x1, waiting for transfers between devices: 53.9 us -> 0.02 us  [local(): lax.psum_scatter(up_grad, 'dp', scatter_dimension=0, tiled=True)]
    reduce_scatter x1, waiting for transfers between devices: 39.7 us -> 0.02 us  [local(): lax.psum_scatter(out_grad, 'dp', scatter_dimension=0, tiled=True)]
    reduce_scatter x1, waiting for transfers between devices: 9.84 us -> 38.4 us  [local(): lax.psum_scatter(mixed_weight_grad, 'dp', scatter_dimension=0, tiled=True)]
    reduce_scatter x4, waiting for transfers between devices: 225 us -> 207 us  [spread_rows(): lax.psum_scatter(term(jnp.int32(0), row_count * lax.axis_size('tensor'))....]
  transfers between devices with their start and end apart: 14 -> 22, of which waited for: 12 -> 17; matrix products, arithmetic and copies ran while one was open for 10% -> 29% of each run, Pallas kernels for 0% -> 0%
where the time goes in v1:
time: 1110 us; the launch traced here: 1100 us
  waiting for transfers between devices  452 us (41%)
  matrix products  259 us (23%)
  local copies, waits for them, and re-layouts  111 us (10%)
  other arithmetic  107 us (10%)
  starting transfers between devices  82.5 us (7%)
  blocking collectives  71 us (6%)
  between operations  16.1 us (1%)
    reduce_scatter x4, waiting for transfers between devices, spread_rows(): lax.psum_scatter(term(jnp.int32(0), row_count * lax.axis_size('tensor'))....  207 us
    ppermute x8, waiting for transfers between devices, ring_gather(): lax.ppermute(going_up, axis, [(d, (d + 1) % ways) for d in range(ways)])  181 us
    ppermute x8, starting transfers between devices, ring_gather(): lax.ppermute(going_up, axis, [(d, (d + 1) % ways) for d in range(ways)])  67.9 us
    unnamed x90, local copies, waits for them, and re-layouts  62.4 us
    convert_element_type x4, other arithmetic, block_backward(): score_grad = (attention * (product - jnp.sum(attention * product, axis=-1...  42.8 us
    psum x1, blocking collectives, local(): lax.psum(jnp.stack([gain_one, shift_one, gain_two, shift_two]), ('dp', 't...  40.4 us
    reduce_scatter x1, waiting for transfers between devices, local(): lax.psum_scatter(mixed_weight_grad, 'dp', scatter_dimension=0, tiled=True)  38.4 us
    dot_general x4, matrix products, block_backward(): jnp.einsum('qhe,khe->hqk', upstream, value_rows, preferred_element_type=j...  38 us
  transfers between devices with their start and end apart: 22, of which 17 were waited for; matrix products, arithmetic and copies ran while one was open for 29% of the time, Pallas kernels for 0%

profile of v1, /device:TPU:0, one launch (start us, length us, event | category | flops | bytes accessed | tf_op | source)
XLA Modules:
  0.0 1098.5 jit_solution(18283304996161773574)
XLA Ops:
  12.4 24.2 %collective-permute-done = bf16[512,1024]{1,0:T(8,128)(2,1)S(1)} collective-permute-done((bf16[512,1024]{1,0:T(8,128)(2,1)}, bf16[512,1024]{1,0:T(8,128)(2,1)S(1)}, u32[]{:S(2)}, u32[]{:S(2)}) %collective-permute-start) | collective-permute-done | bytes 1048608 | tf_op jit(solution)/shard_map/ppermute | solution.py:27
  37.4 20.5 %collective-permute-done.1 = bf16[512,1024]{1,0:T(8,128)(2,1)S(1)} collective-permute-done((bf16[512,1024]{1,0:T(8,128)(2,1)}, bf16[512,1024]{1,0:T(8,128)(2,1)S(1)}, u32[]{:S(2)}, u32[]{:S(2)}) %collective-permute-start.1) | collective-permute-done | bytes 1048608 | tf_op jit(solution)/shard_map/ppermute | solution.py:30
  58.0 22.8 %collective-permute-done.2 = bf16[512,1024]{1,0:T(8,128)(2,1)} collective-permute-done((bf16[512,1024]{1,0:T(8,128)(2,1)S(1)}, bf16[512,1024]{1,0:T(8,128)(2,1)}, u32[]{:S(2)}, u32[]{:S(2)}) %collective-permute-start.2) | collective-permute-done | bytes 1048608 | tf_op jit(solution)/shard_map/ppermute | solution.py:27
  92.9 52.3 %while.28 = (s32[]{:T(128)}, bf16[4,512,4,64]{1,3,2,0:T(8,128)(2,1)}, f32[4,4,512]{2,1,0:T(4,128)}, bf16[4,512,4,64]{1,3,2,0:T(8,128)(2,1)S(1)}, bf16[2048,4,64]...) while((s32[]{:T(128)}, bf16[4,512,4,64]{1,3,2,0:T(8,128)(2,1)}, ...), condition=%wide.region_3.4_spmd.clone, body=%wide.region_0.3_spmd.clone.sunk | while | flops 1124204544 | bytes 53026924 | solution.py:122
  154.4 75.6 %reduce-scatter.9.cloned.1.call-done = bf16[512,1024]{1,0:T(8,128)(2,1)} async-done(((bf16[2048,1024]{1,0:T(8,128)(2,1)}), bf16[512,1024]{1,0:T(8,128)(2,1)}) %reduce-scatter.9.cloned.1.call-update) | async-done | bytes 1048592 | tf_op jit(solution)/shard_map/reduce_scatter | solution.py:82
  238.4 24.1 %collective-permute-done.3 = bf16[512,1024]{1,0:T(8,128)(2,1)S(1)} collective-permute-done((bf16[512,1024]{1,0:T(8,128)(2,1)S(1)}, bf16[512,1024]{1,0:T(8,128)(2,1)S(1)}, u32[]{:S(2)}, u32[]{:S(2)}) %collective-permute-start.3) | collective-permute-done | bytes 1048608 | tf_op jit(solution)/shard_map/ppermute | solution.py:27
  262.5 20.0 %collective-permute-start.5 = (bf16[512,1024]{1,0:T(8,128)(2,1)S(1)}, bf16[512,1024]{1,0:T(8,128)(2,1)S(1)}, u32[]{:S(2)}, u32[]{:S(2)}) collective-permute-start(bf16[512,1024]{1,0:T(8,128)(2,1)S(1)} %collective-permute-done.3), channel_id=1, source_target_pairs={{0,1},{1,2},{2,3},{3,0},{4,5},{5,6},{6,7},{7,4},{8,9},{9,10},{10,1... | collective-permute-start | bytes 3145736 | tf_op jit(solution)/shard_map/ppermute | solution.py:27
  284.7 21.3 %collective-permute-done.5 = bf16[512,1024]{1,0:T(8,128)(2,1)S(1)} collective-permute-done((bf16[512,1024]{1,0:T(8,128)(2,1)S(1)}, bf16[512,1024]{1,0:T(8,128)(2,1)S(1)}, u32[]{:S(2)}, u32[]{:S(2)}) %collective-permute-start.5) | collective-permute-done | bytes 1048608 | tf_op jit(solution)/shard_map/ppermute | solution.py:27
  306.1 26.6 %multiply_convert_fusion.1 = (bf16[2048,1024]{1,0:T(8,128)(2,1)S(1)}, f32[2048,1024]{1,0:T(8,128)}, f32[2048,1024]{1,0:T(8,128)}) fusion(bf16[2048,1024]{1,0:T(8,128)(2,1)S(1)} %constant_dynamic-update-slice_fusion.8, bf16[1024,3072]{1,0:T(8,128)(2,1)S(1)} %bitcast.259), kind=kOutput, calls=%fused_computation.55 | convolution fusion | flops 4431282176 | bytes 27262976 | tf_op jit(solution)/shard_map/dot_general | solution.py:217
  341.8 75.5 %reduce-scatter.11.cloned.1.call-done = bf16[512,1024]{1,0:T(8,128)(2,1)} async-done(((bf16[2048,1024]{1,0:T(8,128)(2,1)}), bf16[512,1024]{1,0:T(8,128)(2,1)}) %reduce-scatter.11.cloned.1.call-update) | async-done | bytes 1048592 | tf_op jit(solution)/shard_map/reduce_scatter | solution.py:82
  428.8 24.1 %collective-permute-done.6 = bf16[512,1024]{1,0:T(8,128)(2,1)S(1)} collective-permute-done((bf16[512,1024]{1,0:T(8,128)(2,1)S(1)}, bf16[512,1024]{1,0:T(8,128)(2,1)S(1)}, u32[]{:S(2)}, u32[]{:S(2)}) %collective-permute-start.6) | collective-permute-done | bytes 1048608 | tf_op jit(solution)/shard_map/ppermute | solution.py:27
  452.9 20.2 %collective-permute-start.8 = (bf16[512,1024]{1,0:T(8,128)(2,1)S(1)}, bf16[512,1024]{1,0:T(8,128)(2,1)S(1)}, u32[]{:S(2)}, u32[]{:S(2)}) collective-permute-start(bf16[512,1024]{1,0:T(8,128)(2,1)S(1)} %collective-permute-done.6), channel_id=1, source_target_pairs={{0,1},{1,2},{2,3},{3,0},{4,5},{5,6},{6,7},{7,4},{8,9},{9,10},{10,1... | collective-permute-start | bytes 3145736 | tf_op jit(solution)/shard_map/ppermute | solution.py:27
  475.2 21.2 %collective-permute-done.8 = bf16[512,1024]{1,0:T(8,128)(2,1)S(1)} collective-permute-done((bf16[512,1024]{1,0:T(8,128)(2,1)S(1)}, bf16[512,1024]{1,0:T(8,128)(2,1)S(1)}, u32[]{:S(2)}, u32[]{:S(2)}) %collective-permute-start.8) | collective-permute-done | bytes 1048608 | tf_op jit(solution)/shard_map/ppermute | solution.py:27
  496.5 12.5 %add_convert_fusion = bf16[2048,1024]{1,0:T(8,128)(2,1)S(1)} fusion(f32[2048,1024]{1,0:T(8,128)} %get-tuple-element.309, f32[2048,1024]{1,0:T(8,128)} %get-tuple-element.329, bf16[2048,1024]{1,0:T(8,128)(2,1)S(1)} %constant_dynamic-update-slice_fusion.4, bf16[1024,3072]{1,0:T(8,128)(2,1)S(1)} %bitcast.261), kind=kOutput, calls=%fused_computation.54 | convolution fusion | flops 4324327424 | bytes 27262976 | tf_op jit(solution)/shard_map/dot_general | solution.py:232
  538.0 55.7 %reduce-scatter.13.cloned.1.call-done = bf16[512,1024]{1,0:T(8,128)(2,1)} async-done(((bf16[2048,1024]{1,0:T(8,128)(2,1)}), bf16[512,1024]{1,0:T(8,128)(2,1)}) %reduce-scatter.13.cloned.1.call-update) | async-done | bytes 1048592 | tf_op jit(solution)/shard_map/reduce_scatter | solution.py:82
  606.1 24.1 %collective-permute-done.9 = bf16[512,1024]{1,0:T(8,128)(2,1)S(1)} collective-permute-done((bf16[512,1024]{1,0:T(8,128)(2,1)S(1)}, bf16[512,1024]{1,0:T(8,128)(2,1)S(1)}, u32[]{:S(2)}, u32[]{:S(2)}) %collective-permute-start.9) | collective-permute-done | bytes 1048608 | tf_op jit(solution)/shard_map/ppermute | solution.py:27
  630.2 20.0 %collective-permute-start.11 = (bf16[512,1024]{1,0:T(8,128)(2,1)S(1)}, bf16[512,1024]{1,0:T(8,128)(2,1)S(1)}, u32[]{:S(2)}, u32[]{:S(2)}) collective-permute-start(bf16[512,1024]{1,0:T(8,128)(2,1)S(1)} %collective-permute-done.9), channel_id=1, source_target_pairs={{0,1},{1,2},{2,3},{3,0},{4,5},{5,6},{6,7},{7,4},{8,9},{9,10},{10,1... | collective-permute-start | bytes 3145736 | tf_op jit(solution)/shard_map/ppermute | solution.py:27
  654.6 19.1 %collective-permute-done.11 = bf16[512,1024]{1,0:T(8,128)(2,1)S(1)} collective-permute-done((bf16[512,1024]{1,0:T(8,128)(2,1)S(1)}, bf16[512,1024]{1,0:T(8,128)(2,1)S(1)}, u32[]{:S(2)}, u32[]{:S(2)}) %collective-permute-start.11) | collective-permute-done | bytes 1048608 | tf_op jit(solution)/shard_map/ppermute | solution.py:27
  687.9 169.5 %while.29 = (s32[]{:T(128)}, f32[2048,4,64]{0,2,1:T(8,128)}, f32[2048,4,64]{0,2,1:T(8,128)}, bf16[4,512,4,64]{1,3,2,0:T(8,128)(2,1)}, bf16[4,512,4,64]{1,3,2,0:T...) while((s32[]{:T(128)}, f32[2048,4,64]{0,2,1:T(8,128)}, ...), condition=%wide.region_17.18_spmd.clone, body=%wide.region_15.17_spmd.clone.sunk | while | flops 2750152704 | bytes 172294320 | solution.py:168
  707.9 10.9 multiply_convert_fusion.4
  875.3 38.4 %reduce-scatter.17.cloned.1.call-done = f32[128,768]{1,0:T(8,128)} async-done(((f32[1024,768]{1,0:T(8,128)}), f32[128,768]{1,0:T(8,128)}) %reduce-scatter.17.cloned.1.call-update) | async-done | bytes 393232 | tf_op jit(solution)/shard_map/reduce_scatter | solution.py:259
  959.4 12.7 %subtract_multiply_fusion = (f32[1,1024,1024]{1,2,0:T(8,128)}, f32[1,1024,1024]{1,2,0:T(8,128)}, f32[1,1024,1024]{1,2,0:T(8,128)}, f32[128,8,8,128]{3,1,2,0:T(8,128)S(1)}, f32[128,8,8,128]{3,1,2,0:T(8,128)S(1)}) fusion(f32[1,1024,1024]{1,2,0:T(8,128)} %copy.87, f32[1024]{0:T(1024)S(1)} %bitcast.266, f32[1,1024,1024]{1,2,0:T(8,128)} %reshape_reshape.3, ...), kind=kLoop, calls=%fused_computation.81 | loop fusion | flops 18874368 | bytes 37752832 | tf_op jit(solution)/shard_map/mul | solution.py:73
  983.1 30.6 %all_to_all.10 = bf16[8,128,4,256]{3,1,2,0:T(8,128)(2,1)S(1)} all-to-all(bf16[8,128,4,256]{3,1,2,0:T(8,128)(2,1)S(1)} %copy.89), channel_id=1, replica_groups=mesh['dp'=8,'tensor'=4] {'dp'}, dimensions={0} | all-to-all | bytes 4194304 | tf_op jit(solution)/shard_map/all_to_all | solution.py:297
  1017.9 40.4 %psum.7 = f32[4,1024]{1,0:T(4,128)S(1)} all-reduce(f32[4,1024]{1,0:T(4,128)S(1)} %pad_maximum_fusion.4), channel_id=1, replica_groups=mesh['dp'=8,'tensor'=4] {'dp','tensor'}, use_global_device_ids=true, to_apply=%region_30.31 | all-reduce | flops 4096 | bytes 32768 | tf_op jit(solution)/shard_map/psum | solution.py:265
  (268 shorter events, 441.7 us)
Async XLA Ops:
  7.2 222.8 %reduce-scatter.9.cloned.1.call-start = ((), (), s32[]{:S(2)}) async-start(), calls=%async_computation.10 | async-start | bytes 5242880 | tf_op jit(solution)/shard_map/reduce_scatter | solution.py:82
  7.2 29.4 %collective-permute-start = (bf16[512,1024]{1,0:T(8,128)(2,1)}, bf16[512,1024]{1,0:T(8,128)(2,1)S(1)}, u32[]{:S(2)}, u32[]{:S(2)}) collective-permute-start(bf16[512,1024]{1,0:T(8,128)(2,1)} %bitcast.237), channel_id=1, source_target_pairs={{0,1},{1,2},{2,3},{3,0},{4,5},{5,6},{6,7},{7,4},{8,9},{9,10},{10,1... | collective-permute-start | bytes 3145736 | tf_op jit(solution)/shard_map/ppermute | solution.py:27
  10.3 47.5 %collective-permute-start.1 = (bf16[512,1024]{1,0:T(8,128)(2,1)}, bf16[512,1024]{1,0:T(8,128)(2,1)S(1)}, u32[]{:S(2)}, u32[]{:S(2)}) collective-permute-start(bf16[512,1024]{1,0:T(8,128)(2,1)} %bitcast.238), channel_id=1, source_target_pairs={{0,3},{1,0},{2,1},{3,2},{4,7},{5,4},{6,5},{7,6},{8,11},{9,8},{10,9... | collective-permute-start | bytes 3145736 | tf_op jit(solution)/shard_map/ppermute | solution.py:30
  36.6 44.2 %collective-permute-start.2 = (bf16[512,1024]{1,0:T(8,128)(2,1)S(1)}, bf16[512,1024]{1,0:T(8,128)(2,1)}, u32[]{:S(2)}, u32[]{:S(2)}) collective-permute-start(bf16[512,1024]{1,0:T(8,128)(2,1)S(1)} %collective-permute-done), channel_id=1, source_target_pairs={{0,1},{1,2},{2,3},{3,0},{4,5},{5,6},{6,7},{7,4},{8,9},{9,10},{10,1... | collective-permute-start | bytes 3145736 | tf_op jit(solution)/shard_map/ppermute | solution.py:27
  153.7 76.3 %copy-start.5 = (bf16[512,1,1024]{2,0,1:T(8,128)(2,1)S(1)}, bf16[512,1,1024]{2,0,1:T(8,128)(2,1)}, u32[]{:S(2)}) copy-start(bf16[512,1,1024]{2,0,1:T(8,128)(2,1)} %param.17) | copy-start | bytes 3145732
  153.7 263.6 %reduce-scatter.11.cloned.1.call-start = ((), (), s32[]{:S(2)}) async-start(), calls=%async_computation.11 | async-start | bytes 5242880 | tf_op jit(solution)/shard_map/reduce_scatter | solution.py:82
  234.5 28.0 %collective-permute-start.3 = (bf16[512,1024]{1,0:T(8,128)(2,1)S(1)}, bf16[512,1024]{1,0:T(8,128)(2,1)S(1)}, u32[]{:S(2)}, u32[]{:S(2)}) collective-permute-start(bf16[512,1024]{1,0:T(8,128)(2,1)S(1)} %get-tuple-element.311), channel_id=1, source_target_pairs={{0,1},{1,2},{2,3},{3,0},{4,5},{5,6},{6,7},{7,4},{8,9},{9,10},{10,1... | collective-permute-start | bytes 3145736 | tf_op jit(solution)/shard_map/ppermute | solution.py:27
  236.0 48.6 %collective-permute-start.4 = (bf16[512,1024]{1,0:T(8,128)(2,1)S(1)}, bf16[512,1024]{1,0:T(8,128)(2,1)S(1)}, u32[]{:S(2)}, u32[]{:S(2)}) collective-permute-start(bf16[512,1024]{1,0:T(8,128)(2,1)S(1)} %get-tuple-element.311), channel_id=1, source_target_pairs={{0,3},{1,0},{2,1},{3,2},{4,7},{5,4},{6,5},{7,6},{8,11},{9,8},{10,9... | collective-permute-start | bytes 3145736 | tf_op jit(solution)/shard_map/ppermute | solution.py:30
  262.5 43.5 %collective-permute-start.5 = (bf16[512,1024]{1,0:T(8,128)(2,1)S(1)}, bf16[512,1024]{1,0:T(8,128)(2,1)S(1)}, u32[]{:S(2)}, u32[]{:S(2)}) collective-permute-start(bf16[512,1024]{1,0:T(8,128)(2,1)S(1)} %collective-permute-done.3), channel_id=1, source_target_pairs={{0,1},{1,2},{2,3},{3,0},{4,5},{5,6},{6,7},{7,4},{8,9},{9,10},{10,1... | collective-permute-start | bytes 3145736 | tf_op jit(solution)/shard_map/ppermute | solution.py:27
  341.0 78.7 %copy-start.19 = (bf16[512,1,1024]{2,0,1:T(8,128)(2,1)S(1)}, bf16[512,1,1024]{2,0,1:T(8,128)(2,1)}, u32[]{:S(2)}) copy-start(bf16[512,1,1024]{2,0,1:T(8,128)(2,1)} %param.20) | copy-start | bytes 3145732
  341.0 252.7 %reduce-scatter.13.cloned.1.call-start = ((), (), s32[]{:S(2)}) async-start(), calls=%async_computation.12 | async-start | bytes 5242880 | tf_op jit(solution)/shard_map/reduce_scatter | solution.py:82
  425.0 27.9 %collective-permute-start.6 = (bf16[512,1024]{1,0:T(8,128)(2,1)S(1)}, bf16[512,1024]{1,0:T(8,128)(2,1)S(1)}, u32[]{:S(2)}, u32[]{:S(2)}) collective-permute-start(bf16[512,1024]{1,0:T(8,128)(2,1)S(1)} %get-tuple-element.304), channel_id=1, source_target_pairs={{0,1},{1,2},{2,3},{3,0},{4,5},{5,6},{6,7},{7,4},{8,9},{9,10},{10,1... | collective-permute-start | bytes 3145736 | tf_op jit(solution)/shard_map/ppermute | solution.py:27
  426.4 48.6 %collective-permute-start.7 = (bf16[512,1024]{1,0:T(8,128)(2,1)S(1)}, bf16[512,1024]{1,0:T(8,128)(2,1)S(1)}, u32[]{:S(2)}, u32[]{:S(2)}) collective-permute-start(bf16[512,1024]{1,0:T(8,128)(2,1)S(1)} %get-tuple-element.304), channel_id=1, source_target_pairs={{0,3},{1,0},{2,1},{3,2},{4,7},{5,4},{6,5},{7,6},{8,11},{9,8},{10,9... | collective-permute-start | bytes 3145736 | tf_op jit(solution)/shard_map/ppermute | solution.py:30
  452.9 43.5 %collective-permute-start.8 = (bf16[512,1024]{1,0:T(8,128)(2,1)S(1)}, bf16[512,1024]{1,0:T(8,128)(2,1)S(1)}, u32[]{:S(2)}, u32[]{:S(2)}) collective-permute-start(bf16[512,1024]{1,0:T(8,128)(2,1)S(1)} %collective-permute-done.6), channel_id=1, source_target_pairs={{0,1},{1,2},{2,3},{3,0},{4,5},{5,6},{6,7},{7,4},{8,9},{9,10},{10,1... | collective-permute-start | bytes 3145736 | tf_op jit(solution)/shard_map/ppermute | solution.py:27
  517.4 357.8 %reduce-scatter.21.cloned.1.call-start = ((), (), s32[]{:S(2)}) async-start(), calls=%async_computation.16 | async-start | bytes 4718592 | tf_op jit(solution)/shard_map/reduce_scatter | solution.py:261
  527.4 347.8 %reduce-scatter.23.cloned.1.call-start = ((), (), s32[]{:S(2)}) async-start(), calls=%async_computation.17 | async-start | bytes 4718592 | tf_op jit(solution)/shard_map/reduce_scatter | solution.py:262
  538.0 337.3 %reduce-scatter.19.cloned.1.call-start = ((), (), s32[]{:S(2)}) async-start(), calls=%async_computation.15 | async-start | bytes 1179648 | tf_op jit(solution)/shard_map/reduce_scatter | solution.py:260
  602.3 27.9 %collective-permute-start.9 = (bf16[512,1024]{1,0:T(8,128)(2,1)S(1)}, bf16[512,1024]{1,0:T(8,128)(2,1)S(1)}, u32[]{:S(2)}, u32[]{:S(2)}) collective-permute-start(bf16[512,1024]{1,0:T(8,128)(2,1)S(1)} %get-tuple-element.301), channel_id=1, source_target_pairs={{0,1},{1,2},{2,3},{3,0},{4,5},{5,6},{6,7},{7,4},{8,9},{9,10},{10,1... | collective-permute-start | bytes 3145736 | tf_op jit(solution)/shard_map/ppermute | solution.py:27
  603.8 48.6 %collective-permute-start.10 = (bf16[512,1024]{1,0:T(8,128)(2,1)S(1)}, bf16[512,1024]{1,0:T(8,128)(2,1)}, u32[]{:S(2)}, u32[]{:S(2)}) collective-permute-start(bf16[512,1024]{1,0:T(8,128)(2,1)S(1)} %get-tuple-element.301), channel_id=1, source_target_pairs={{0,3},{1,0},{2,1},{3,2},{4,7},{5,4},{6,5},{7,6},{8,11},{9,8},{10,9... | collective-permute-start | bytes 3145736 | tf_op jit(solution)/shard_map/ppermute | solution.py:30
  630.2 43.5 %collective-permute-start.11 = (bf16[512,1024]{1,0:T(8,128)(2,1)S(1)}, bf16[512,1024]{1,0:T(8,128)(2,1)S(1)}, u32[]{:S(2)}, u32[]{:S(2)}) collective-permute-start(bf16[512,1024]{1,0:T(8,128)(2,1)S(1)} %collective-permute-done.9), channel_id=1, source_target_pairs={{0,1},{1,2},{2,3},{3,0},{4,5},{5,6},{6,7},{7,4},{8,9},{9,10},{10,1... | collective-permute-start | bytes 3145736 | tf_op jit(solution)/shard_map/ppermute | solution.py:27
  686.6 227.0 %reduce-scatter.17.cloned.1.call-start = ((), (), s32[]{:S(2)}) async-start(), calls=%async_computation.14 | async-start | bytes 3538944 | tf_op jit(solution)/shard_map/reduce_scatter | solution.py:259
  867.7 212.9 %reduce-scatter.15.cloned.1.call-start = ((), (), s32[]{:S(2)}) async-start(), calls=%async_computation.13 | async-start | bytes 5242880 | tf_op jit(solution)/shard_map/reduce_scatter | solution.py:82
  922.6 31.0 %all-to-all-start = ((bf16[8,128,4,256]{3,1,2,0:T(8,128)(2,1)}), bf16[8,128,4,256]{3,1,2,0:T(8,128)(2,1)}, u32[]{:S(2)}, u32[]{:S(2)}) async-start(bf16[8,128,4,256]{3,1,2,0:T(8,128)(2,1)} %copy.82), calls=%async_computation.8 | async-start | bytes 4194304 | tf_op jit(solution)/shard_map/all_to_all | solution.py:282
  927.0 156.2 %all-gather.2.cloned.1.call-start = ((), (), s32[]{:S(2)}) async-start(), calls=%async_computation.18 | async-start | bytes 7077888 | tf_op jit(solution)/shard_map/all_gather | solution.py:302
  (39 other events, 834.5 us)
Sparse Core Ops, SparseCore 0:
  153.8 76.1 reduce-scatter.8
  341.1 76.1 reduce-scatter.10
  517.5 76.1 reduce-scatter.12
  596.9 51.6 reduce-scatter.20
  652.4 51.1 reduce-scatter.22
  706.6 35.9 reduce-scatter.18
  867.8 45.7 reduce-scatter.16
  916.5 76.7 reduce-scatter.14
  1016.7 46.6 all-gather.1
